TPU v7x, 32 devices: a whole 2x2x4 slice. The times are simulated.
32 devices in a mesh: ep: 16 (over z, y, x), dp: 2 (over core).
Axes of the slice: x: 2, y: 2, z: 4, core: 2. Of those that a mesh axis runs over, the one named last changes fastest.
Arguments:
- tokens: bfloat16 [2048, 2048], P(('dp', 'ep')), parts along dimension 0, may hold values from -6 to 6
- expert_ids: int32 [2048, 8], P(('dp', 'ep')), parts along dimension 0, may hold values from 0 to 15, all different within a row; in each aligned block of 64 rows (0 to 63, 64 to 127, ...) at most 64 rows name the same one
- gate_probs: float32 [2048, 8], P(('dp', 'ep')), parts along dimension 0, may hold values from 0.05 to 1
- w_gate: bfloat16 [16, 2048, 768], P('ep'), may hold values from -0.125 to 0.125
- w_up: bfloat16 [16, 2048, 768], P('ep'), may hold values from -0.125 to 0.125
- w_down: bfloat16 [16, 768, 2048], P('ep'), may hold values from -0.21875 to 0.21875
Outputs:
- combined: bfloat16 [2048, 2048], P(('dp', 'ep')), parts along dimension 0
There are 2 independent parts, one for each index of `dp`. A program takes and returns all parts, laid end to end along the dimension named above; an argument that names none is the same for every part. Nothing has to cross between parts.
Inputs may be any that keep to these rules, and one draw needn't show every extreme that they name: `expert_ids`: each row names 8 different experts. Among the rows of one index of ep (aligned blocks of 64 rows) no expert is named by more than 64 rows, and in every draw some expert is named by exactly 64 rows of some block. Expert popularity is skewed.
All inputs are finite; a program needn't handle non-finite values.
Results may differ from a plain program's by a relative error of at most 0.0085.
Values may be sent and summed in bfloat16 or wider, within the bound.
A program may use at most 64 MiB of HBM per device.

v0:
```python
import jax
import jax.numpy as jnp
from jax import lax
from jax.sharding import PartitionSpec as P


def expert_ffn(row_block, gate_matrix, up_matrix, down_matrix):
    gate_act = jnp.dot(row_block, gate_matrix, preferred_element_type=jnp.float32)
    up_act = jnp.dot(row_block, up_matrix, preferred_element_type=jnp.float32)
    hidden = (jax.nn.silu(gate_act) * up_act).astype(jnp.bfloat16)
    return jnp.dot(hidden, down_matrix, preferred_element_type=jnp.float32).astype(jnp.bfloat16)


def shards(tokens, expert_ids, gate_probs, w_gate, w_up, w_down):
    ep_count = lax.axis_size("ep")
    tok_count, features = tokens.shape
    top_count = expert_ids.shape[1]
    most = min(tok_count, 2 * tok_count * top_count // ep_count)
    gate_matrix = w_gate[0]
    up_matrix = w_up[0]
    down_matrix = w_down[0]
    flat_ids = expert_ids.reshape(-1)
    owners = jnp.arange(tok_count * top_count, dtype=jnp.int32) // top_count
    onehot = (flat_ids[:, None] == jnp.arange(ep_count, dtype=jnp.int32)[None, :]).astype(jnp.int32)
    within_rank = jnp.sum((jnp.cumsum(onehot, axis=0) - onehot) * onehot, axis=1)
    slot_index = flat_ids * most + within_rank
    slot_token = jnp.zeros((ep_count * most,), jnp.int32).at[slot_index].set(owners)
    filled = jnp.zeros((ep_count * most,), jnp.bool_).at[slot_index].set(True)
    send_rows = jnp.where(filled[:, None], tokens[slot_token], jnp.zeros((), jnp.bfloat16))
    send_rows = send_rows.reshape(ep_count, most, features)

    def serve_rows(received):
        flat_out = expert_ffn(received.reshape(-1, features), gate_matrix, up_matrix, down_matrix)
        return flat_out.reshape(received.shape)

    half_width = most // 2
    returned_parts = []
    for block_index in range(2):
        part_rows = send_rows[:, block_index * half_width : (block_index + 1) * half_width]
        received = lax.all_to_all(part_rows, "ep", split_axis=0, concat_axis=0, tiled=True)
        served = serve_rows(received)
        returned_parts.append(lax.all_to_all(served, "ep", split_axis=0, concat_axis=0, tiled=True))
    gathered = jnp.concatenate(returned_parts, axis=1)
    picked = gathered.reshape(-1, features)[slot_index].reshape(tok_count, top_count, features)
    weights = gate_probs / jnp.sum(gate_probs, axis=1, keepdims=True)
    combined = jnp.einsum("tk,tkd->td", weights, picked.astype(jnp.float32))
    return combined.astype(jnp.bfloat16)


def solution(mesh):
    placed = (
        P(("dp", "ep"), None),
        P(("dp", "ep"), None),
        P(("dp", "ep"), None),
        P("ep", None, None),
        P("ep", None, None),
        P("ep", None, None),
    )
    return jax.shard_map(
        shards, mesh=mesh, in_specs=placed, out_specs=P(("dp", "ep"), None), check_vma=False
    )
```

profile of v0, /device:TPU:0, one launch (start us, length us, event | category | flops | bytes accessed | tf_op | source)
XLA Modules:
  0.0 244.8 jit_solution(4292989066528647094)
XLA Ops:
  0.0 0.0 copy-start
  0.0 0.0 copy-start.1
  0.0 0.9 copy.8
  0.9 0.1 eq.29
  1.0 0.1 eq.25
  1.1 0.7 broadcast_multiply_fusion
  1.8 1.2 reduce-window.6
  3.0 0.2 slice_reduce_fusion
  3.2 0.1 copy.7
  3.3 0.1 mul.34
  3.4 0.1 fusion.30
  3.5 2.4 scatter_custom_fusion.1
  6.0 2.4 scatter_custom_fusion
  8.5 0.1 broadcast_in_dim.31
  8.5 0.0 copy-done.1
  8.5 6.0 %gather_fusion = bf16[1024,2048]{1,0:T(8,128)(2,1)} fusion(bf16[64,2048]{1,0:T(8,128)(2,1)S(1)} %copy-done.1, s32[1024]{0:T(1024)S(1)} %fusion.32), kind=kCustom, calls=%fused_computation | custom fusion | bytes 8392704 | tf_op jit(solution)/shard_map/gather | solution.py:29
  14.6 2.5 %broadcast_select_fusion = bf16[16,64,2048]{2,1,0:T(8,128)(2,1)S(1)} fusion(bf16[16,64,2048]{2,1,0:T(8,128)(2,1)} %bitcast.68, pred[16,64]{1,0:T(8,128)(4,1)S(1)} %broadcast_in_dim.31), kind=kLoop, calls=%fused_computation.5 | loop fusion | flops 2097152 | bytes 8389632 | tf_op jit(solution)/shard_map/jit(_where)/select_n | solution.py:29
  17.1 1.7 fusion.42
  18.8 57.1 %all_to_all.20 = bf16[16,32,2048]{2,1,0:T(8,128)(2,1)} all-to-all(bf16[16,32,2048]{2,1,0:T(8,128)(2,1)S(1)} %get-tuple-element.5), channel_id=1, replica_groups=mesh['ep'=16,'dp'=2] {'ep'}, dimensions={0} | all-to-all | bytes 4194304 | tf_op jit(solution)/shard_map/all_to_all | solution.py:40
  75.9 5.0 %all-to-all-start.2 = ((bf16[16,32,2048]{2,1,0:T(8,128)(2,1)}), bf16[16,32,2048]{2,1,0:T(8,128)(2,1)}, u32[]{:S(2)}, u32[]{:S(2)}) async-start(bf16[16,32,2048]{2,1,0:T(8,128)(2,1)} %get-tuple-element.6), calls=%async_computation.2 | async-start | bytes 4194304 | tf_op jit(solution)/shard_map/all_to_all | solution.py:40
  80.9 5.5 %fusion.10 = f32[512,768]{1,0:T(8,128)} fusion(bf16[512,2048]{1,0:T(8,128)(2,1)} %bitcast.71, bf16[1,2048,768]{2,1,0:T(8,128)(2,1)} %param.9), kind=kOutput, calls=%fused_computation.16 | convolution fusion | flops 1610612736 | bytes 6815744 | tf_op jit(solution)/shard_map/dot_general | solution.py:8
  86.5 0.0 copy-done
  86.5 8.2 %fusion.12 = bf16[512,2048]{1,0:T(8,128)(2,1)} fusion(bf16[1,768,2048]{2,1,0:T(8,128)(2,1)S(1)} %copy-done, f32[512,768]{1,0:T(8,128)} %fusion.10, bf16[512,2048]{1,0:T(8,128)(2,1)} %bitcast.72, bf16[1,2048,768]{2,1,0:T(8,128)(2,1)} %param.10), kind=kOutput, calls=%fused_computation.18 | convolution fusion | flops 3224633344 | bytes 12058624 | tf_op jit(solution)/shard_map/dot_general | solution.py:11
  94.7 29.7 %all-to-all-done.2 = bf16[16,32,2048]{2,1,0:T(8,128)(2,1)} async-done(((bf16[16,32,2048]{2,1,0:T(8,128)(2,1)}), bf16[16,32,2048]{2,1,0:T(8,128)(2,1)}, u32[]{:S(2)}, u32[]{:S(2)}) %all-to-all-start.2) | async-done | bytes 2097184 | tf_op jit(solution)/shard_map/all_to_all | solution.py:40
  124.4 11.1 %all-to-all-start.1 = ((bf16[16,32,2048]{2,1,0:T(8,128)(2,1)}), bf16[16,32,2048]{2,1,0:T(8,128)(2,1)}, u32[]{:S(2)}, u32[]{:S(2)}) async-start(bf16[16,32,2048]{2,1,0:T(8,128)(2,1)} %bitcast.70), calls=%async_computation.1 | async-start | bytes 4194304 | tf_op jit(solution)/shard_map/all_to_all | solution.py:42
  135.5 5.5 %fusion.8 = f32[512,768]{1,0:T(8,128)} fusion(bf16[512,2048]{1,0:T(8,128)(2,1)} %bitcast.10, bf16[1,2048,768]{2,1,0:T(8,128)(2,1)} %param.9), kind=kOutput, calls=%fused_computation.14 | convolution fusion | flops 1610612736 | bytes 6815744 | tf_op jit(solution)/shard_map/dot_general | solution.py:8
  141.1 8.3 %fusion.15 = bf16[512,2048]{1,0:T(8,128)(2,1)} fusion(bf16[1,768,2048]{2,1,0:T(8,128)(2,1)S(1)} %copy-done, f32[512,768]{1,0:T(8,128)} %fusion.8, bf16[512,2048]{1,0:T(8,128)(2,1)} %bitcast.10, bf16[1,2048,768]{2,1,0:T(8,128)(2,1)} %param.10), kind=kOutput, calls=%fused_computation.19 | convolution fusion | flops 3224633344 | bytes 12058624 | tf_op jit(solution)/shard_map/dot_general | solution.py:11
  149.3 27.6 %all-to-all-done.1 = bf16[16,32,2048]{2,1,0:T(8,128)(2,1)} async-done(((bf16[16,32,2048]{2,1,0:T(8,128)(2,1)}), bf16[16,32,2048]{2,1,0:T(8,128)(2,1)}, u32[]{:S(2)}, u32[]{:S(2)}) %all-to-all-start.1) | async-done | bytes 2097184 | tf_op jit(solution)/shard_map/all_to_all | solution.py:42
  176.9 0.0 copy-start.2
  176.9 11.4 %all-to-all-start.3 = ((bf16[16,32,2048]{2,1,0:T(8,128)(2,1)}), bf16[16,32,2048]{2,1,0:T(8,128)(2,1)}, u32[]{:S(2)}, u32[]{:S(2)}) async-start(bf16[16,32,2048]{2,1,0:T(8,128)(2,1)} %bitcast.69), calls=%async_computation.3 | async-start | bytes 4194304 | tf_op jit(solution)/shard_map/all_to_all | solution.py:42
  188.3 0.0 copy-done.2
  188.4 0.1 copy.11
  188.5 40.4 %all-to-all-done.3 = bf16[16,32,2048]{2,1,0:T(8,128)(2,1)} async-done(((bf16[16,32,2048]{2,1,0:T(8,128)(2,1)}), bf16[16,32,2048]{2,1,0:T(8,128)(2,1)}, u32[]{:S(2)}, u32[]{:S(2)}) %all-to-all-start.3) | async-done | bytes 2097184 | tf_op jit(solution)/shard_map/all_to_all | solution.py:42
  228.9 4.7 %pad_maximum_fusion = bf16[16,64,2048]{2,1,0:T(8,128)(2,1)} fusion(bf16[16,32,2048]{2,1,0:T(8,128)(2,1)} %all-to-all-done.3, bf16[16,32,2048]{2,1,0:T(8,128)(2,1)} %all-to-all-done.1), kind=kLoop, calls=%fused_computation.4 | loop fusion | flops 8388608 | bytes 8388608 | tf_op jit(solution)/shard_map/concatenate | solution.py:43
  233.7 8.0 %gather_fusion.1 = bf16[512,2048]{1,0:T(8,128)(2,1)} fusion(bf16[1024,2048]{1,0:T(8,128)(2,1)} %bitcast.67, s32[1024]{0:T(1024)S(1)} %pad_clamp_fusion), kind=kCustom, calls=%fused_computation.1 | custom fusion | bytes 4196352 | tf_op jit(solution)/shard_map/gather | solution.py:44
  241.7 2.3 fusion.18
  243.9 0.9 copy.16
  (10 shorter events, 0.1 us)
Async XLA Ops:
  0.0 86.5 %copy-start = (bf16[1,768,2048]{2,1,0:T(8,128)(2,1)S(1)}, bf16[1,768,2048]{2,1,0:T(8,128)(2,1)}, u32[]{:S(2)}) copy-start(bf16[1,768,2048]{2,1,0:T(8,128)(2,1)} %param.11) | copy-start | bytes 9437188
  0.0 8.5 %copy-start.1 = (bf16[64,2048]{1,0:T(8,128)(2,1)S(1)}, bf16[64,2048]{1,0:T(8,128)(2,1)}, u32[]{:S(2)}) copy-start(bf16[64,2048]{1,0:T(8,128)(2,1)} %param.6) | copy-start | bytes 786436
  75.9 48.4 %all-to-all-start.2 = ((bf16[16,32,2048]{2,1,0:T(8,128)(2,1)}), bf16[16,32,2048]{2,1,0:T(8,128)(2,1)}, u32[]{:S(2)}, u32[]{:S(2)}) async-start(bf16[16,32,2048]{2,1,0:T(8,128)(2,1)} %get-tuple-element.6), calls=%async_computation.2 | async-start | bytes 4194304 | tf_op jit(solution)/shard_map/all_to_all | solution.py:40
  124.4 52.5 %all-to-all-start.1 = ((bf16[16,32,2048]{2,1,0:T(8,128)(2,1)}), bf16[16,32,2048]{2,1,0:T(8,128)(2,1)}, u32[]{:S(2)}, u32[]{:S(2)}) async-start(bf16[16,32,2048]{2,1,0:T(8,128)(2,1)} %bitcast.70), calls=%async_computation.1 | async-start | bytes 4194304 | tf_op jit(solution)/shard_map/all_to_all | solution.py:42
  176.9 11.4 %copy-start.2 = (f32[64,8]{0,1:T(8,128)S(1)}, f32[64,8]{0,1:T(8,128)}, u32[]{:S(2)}) copy-start(f32[64,8]{0,1:T(8,128)} %param.8) | copy-start | bytes 6148
  176.9 52.0 %all-to-all-start.3 = ((bf16[16,32,2048]{2,1,0:T(8,128)(2,1)}), bf16[16,32,2048]{2,1,0:T(8,128)(2,1)}, u32[]{:S(2)}, u32[]{:S(2)}) async-start(bf16[16,32,2048]{2,1,0:T(8,128)(2,1)} %bitcast.69), calls=%async_computation.3 | async-start | bytes 4194304 | tf_op jit(solution)/shard_map/all_to_all | solution.py:42
where the time goes:
time: 250 us; the launch traced here: 245 us
  waiting for transfers between devices  97.7 us (39%)
  blocking collectives  57.1 us (23%)
  matrix products  29.9 us (12%)
  starting transfers between devices  27.5 us (11%)
  local copies, waits for them, and re-layouts  23.2 us (9%)
  other arithmetic  9.31 us (4%)
    all_to_all x2, waiting for transfers between devices, shards(): lax.all_to_all(served, 'ep', split_axis=0, concat_axis=0, tiled=True)  68 us
    all_to_all x1, blocking collectives, shards(): lax.all_to_all(part_rows, 'ep', split_axis=0, concat_axis=0, tiled=True)  57.1 us
    all_to_all x1, waiting for transfers between devices, shards(): lax.all_to_all(part_rows, 'ep', split_axis=0, concat_axis=0, tiled=True)  29.7 us
    all_to_all x2, starting transfers between devices, shards(): lax.all_to_all(served, 'ep', split_axis=0, concat_axis=0, tiled=True)  22.5 us
    dot_general x2, matrix products, expert_ffn(): jnp.dot(hidden, down_matrix, preferred_element_type=jnp.float32)  16.5 us
    dot_general x2, matrix products, expert_ffn(): jnp.dot(row_block, gate_matrix, preferred_element_type=jnp.float32)  11.1 us
    gather x1, local copies, waits for them, and re-layouts, shards(): gathered.reshape(-1, features)[slot_index]  8 us
    gather x1, local copies, waits for them, and re-layouts, shards(): tokens[slot_token]  6.01 us
  transfers between devices with their start and end apart: 3, of which 3 were waited for; matrix products, arithmetic and copies ran while one was open for 11% of the time, Pallas kernels for 0%

commit v1 on v0

v1 whole, which is shorter than its diff:
```python
import functools

import jax
import jax.numpy as jnp
from jax import lax
from jax.experimental import pallas as pl
from jax.experimental.pallas import tpu as pltpu
from jax.sharding import PartitionSpec as P

LANES = 128
ROWS = 16
TILE = 256


def kernel(n, cfg, tokens, ids, probs, wg_hbm, wu_hbm, wd_hbm, out,
           x_buf, y_buf, r1, r2, r3, gates, hidden, wg, wu, wd,
           ag1_s, ag1_r, agz_s, agz_r, ag3_s, ag3_r,
           rs1_s, rs1_r, rs2_s, rs2_r, rs3_s, rs3_r, loc):
    nz = n // 4
    toks, width = out.shape
    chunks = toks // ROWS
    half = width // 2
    ff = wg.shape[1]
    me = lax.axis_index("ep")
    x, y, z = me % 2, (me // 2) % 2, me // 4
    up, down = z < nz - 1, z > 0
    dev = lambda zz, yy, xx: {"ep": (zz * 2 + yy) * 2 + xx}
    x_nbr, y_nbr = dev(z, y, 1 - x), dev(z, 1 - y, x)
    up_nbr, down_nbr = dev(jnp.minimum(z + 1, nz - 1), y, x), dev(jnp.maximum(z - 1, 0), y, x)

    wcopies = [pltpu.make_async_copy(a, b, loc.at[chunks + i])
               for i, (a, b) in enumerate(((wg_hbm.at[0], wg), (wu_hbm.at[0], wu), (wd_hbm.at[0], wd)))]
    own = []
    for c in range(chunks):
        cp = pltpu.make_async_copy(tokens.at[c * ROWS:(c + 1) * ROWS],
                                   x_buf.at[c, z, y, x, :, 0:width], loc.at[c])
        cp.start()
        own.append(cp)
    for cp in wcopies:
        cp.start()

    barrier = pltpu.get_barrier_semaphore()
    for nbr in (x_nbr, y_nbr):
        pl.semaphore_signal(barrier, inc=1, device_id=nbr, device_id_type=pl.DeviceIdType.MESH)
    for ok, nbr in ((up, up_nbr), (down, down_nbr)):
        @pl.when(ok)
        def _(nbr=nbr):
            pl.semaphore_signal(barrier, inc=1, device_id=nbr, device_id_type=pl.DeviceIdType.MESH)

    p = probs[...]
    w = p / jnp.sum(p, axis=1, keepdims=True)
    lane = lax.broadcasted_iota(jnp.int32, (toks, LANES), 1)
    named = jnp.where(lane < n, lane, lane - n)
    g = jnp.zeros((toks, LANES), jnp.float32)
    for k in range(ids.shape[1]):
        g = g + jnp.where(ids[:, k:k + 1] == named, w[:, k:k + 1], 0.0)
    hi = g.astype(jnp.bfloat16).astype(jnp.float32)
    gates[...] = jnp.where(lane < n, hi, g - hi).astype(jnp.bfloat16)
    gcopies = []
    for c in range(chunks):
        cp = pltpu.make_async_copy(gates.at[c * ROWS:(c + 1) * ROWS],
                                   x_buf.at[c, z, y, x, :, width:width + LANES], loc.at[chunks + 3 + c])
        cp.start()
        gcopies.append(cp)

    pl.semaphore_wait(barrier, 2 + up.astype(jnp.int32) + down.astype(jnp.int32))

    sends = []

    def send(src, dst, ssem, rsem, nbr, ok=None):
        cp = pltpu.make_async_remote_copy(src_ref=src, dst_ref=dst, send_sem=ssem, recv_sem=rsem,
                                          device_id=nbr, device_id_type=pl.DeviceIdType.MESH)
        if ok is None:
            cp.start()
        else:
            pl.when(ok)(cp.start)
        sends.append((cp, ok))

    def landed(dst, rsem):
        pltpu.make_async_copy(dst, dst, rsem).wait()

    cols = (slice(0, half), slice(half, width + LANES))
    ycols = (slice(0, half), slice(half, width))
    first_nbr, last_nbr = (x_nbr, y_nbr), (y_nbr, x_nbr)

    def group(buf, c, h, zz, cs, other=False):
        if h == 0:
            return buf.at[c, zz, (1 - y) if other else y, :, :, cs[0]]
        return buf.at[c, zz, :, (1 - x) if other else x, :, cs[1]]

    def ag_first(c):
        own[c].wait()
        gcopies[c].wait()
        for h in range(2):
            blk = x_buf.at[c, z, y, x, :, cols[h]]
            send(blk, blk, ag1_s.at[c, h], ag1_r.at[c, h], first_nbr[h])

    def ag_last(c, h, zz, ok=None):
        blk = group(x_buf, c, h, zz, cols)
        send(blk, blk, ag3_s.at[c, h, zz], ag3_r.at[c, h, zz], last_nbr[h], ok)

    def ag_step(c, d):
        for h in range(2):
            if d == 0:
                mate = (x_buf.at[c, z, y, 1 - x, :, cols[0]], x_buf.at[c, z, 1 - y, x, :, cols[1]])[h]
                landed(mate, ag1_r.at[c, h])
                blk = group(x_buf, c, h, z, cols)
                send(blk, blk, agz_s.at[c, h, 0, z], agz_r.at[c, h, z], up_nbr, up)
                send(blk, blk, agz_s.at[c, h, 1, z], agz_r.at[c, h, z], down_nbr, down)
                ag_last(c, h, z)
            else:
                for way, origin, ok, more, nbr in ((0, z - d, z - d >= 0, up, up_nbr),
                                                   (1, z + d, z + d <= nz - 1, down, down_nbr)):
                    at = jnp.clip(origin, 0, nz - 1)
                    blk = group(x_buf, c, h, at, cols)
                    pl.when(ok)(functools.partial(landed, blk, agz_r.at[c, h, at]))
                    if d < nz - 1:
                        send(blk, blk, agz_s.at[c, h, way, at], agz_r.at[c, h, at], nbr, jnp.logical_and(ok, more))
                    ag_last(c, h, at, ok)

    def ag_end(c):
        for h in range(2):
            for zz in range(nz):
                landed(group(x_buf, c, h, zz, cols, True), ag3_r.at[c, h, zz])

    rows = n * ROWS

    def ffn_in(c):
        if c == 0:
            wcopies[0].wait()
            wcopies[1].wait()
        tail = x_buf[c, :, :, :, :, width:width + LANES].reshape(rows, LANES).astype(jnp.float32)
        lanes = lax.broadcasted_iota(jnp.int32, (rows, LANES), 1)
        mine = jnp.logical_or(lanes == me, lanes == me + n)
        gcol = jnp.sum(jnp.where(mine, tail, 0.0), axis=1, keepdims=True)

        def body(j, carry):
            at = pl.ds(pl.multiple_of(j * TILE, TILE), TILE)
            xs = x_buf[c, :, :, :, :, 0:width].reshape(rows, width)
            ga = jnp.dot(xs, wg[:, at], preferred_element_type=jnp.float32)
            ua = jnp.dot(xs, wu[:, at], preferred_element_type=jnp.float32)
            hidden[:, at] = (ga / (1.0 + jnp.exp(-ga)) * ua * gcol).astype(jnp.bfloat16)
            return carry

        lax.fori_loop(0, ff // TILE, body, 0)

    def ffn_out(c, part, parts):
        if c == 0 and part == 0:
            wcopies[2].wait()
        per = width // TILE // parts

        def body(j, carry):
            at = pl.ds(pl.multiple_of(j * TILE, TILE), TILE)
            o = jnp.dot(hidden[...], wd[:, at], preferred_element_type=jnp.float32)
            y_buf[c, :, :, :, :, at] = o.astype(jnp.bfloat16).reshape(nz, 2, 2, ROWS, TILE)
            return carry

        lax.fori_loop(part * per, (part + 1) * per, body, 0)

    def rs_first(c, h):
        for i in range(nz):
            zz = jnp.where(z >= nz // 2, i, nz - 1 - i)
            send(group(y_buf, c, h, zz, ycols, True), r1.at[c, h, zz], rs1_s.at[c, h, zz],
                 rs1_r.at[c, h, zz], last_nbr[h])

    def add(c, h, zz, bufs):
        mine = group(y_buf, c, h, zz, ycols)
        total = mine[...].astype(jnp.float32)
        for b in bufs:
            total = total + b[...].astype(jnp.float32)
        mine[...] = total.astype(jnp.bfloat16)

    def rs_step(c, s):
        k = nz - 1 - s
        for h in range(2):
            if k > 0:
                for way, dest, ok, prev, nbr in ((0, z + k, z + k <= nz - 1, down, up_nbr),
                                                 (1, z - k, z - k >= 0, up, down_nbr)):
                    at = jnp.clip(dest, 0, nz - 1)

                    @pl.when(ok)
                    def _():
                        landed(r1.at[c, h, at], rs1_r.at[c, h, at])

                        @pl.when(prev)
                        def _():
                            landed(r2.at[c, h, way, at], rs2_r.at[c, h, way, at])
                            add(c, h, at, (r1.at[c, h, at], r2.at[c, h, way, at]))

                        @pl.when(jnp.logical_not(prev))
                        def _():
                            add(c, h, at, (r1.at[c, h, at],))

                    send(group(y_buf, c, h, at, ycols), r2.at[c, h, way, at], rs2_s.at[c, h, way, at],
                         rs2_r.at[c, h, way, at], nbr, ok)
            else:
                landed(r1.at[c, h, z], rs1_r.at[c, h, z])
                add(c, h, z, (r1.at[c, h, z],))
                for way, prev in ((0, down), (1, up)):
                    @pl.when(prev)
                    def _():
                        landed(r2.at[c, h, way, z], rs2_r.at[c, h, way, z])
                        add(c, h, z, (r2.at[c, h, way, z],))
                mate = (y_buf.at[c, z, y, 1 - x, :, ycols[0]], y_buf.at[c, z, 1 - y, x, :, ycols[1]])[h]
                send(mate, r3.at[c, h], rs3_s.at[c, h], rs3_r.at[c, h], first_nbr[h])

    def rs_end(c):
        for h in range(2):
            landed(r3.at[c, h], rs3_r.at[c, h])
            total = y_buf[c, z, y, x, :, ycols[h]].astype(jnp.float32) + r3[c, h].astype(jnp.float32)
            out[c * ROWS:(c + 1) * ROWS, ycols[h]] = total.astype(jnp.bfloat16)

    tasks = []
    step, lag, mm = cfg["step"], cfg["lag"], cfg["mm"]
    for c in range(chunks):
        tasks.append((-1.0 + c * 0.01, functools.partial(ag_first, c)))
        t = c * lag
        for d in range(nz):
            tasks.append((t, functools.partial(ag_step, c, d)))
            t += step
        tasks.append((t, functools.partial(ag_end, c)))
        tasks.append((t + 0.01, functools.partial(ffn_in, c)))
        t += mm
        for part in range(2):
            tasks.append((t + 0.01, functools.partial(ffn_out, c, part, 2)))
            tasks.append((t + 0.02, functools.partial(rs_first, c, part)))
            t += mm / 4
        t += step
        for s in range(nz):
            tasks.append((t, functools.partial(rs_step, c, s)))
            t += step
        tasks.append((t, functools.partial(rs_end, c)))
    for _, task in sorted(tasks, key=lambda item: item[0]):
        task()

    for cp, ok in sends:
        if ok is None:
            cp.wait_send()
        else:
            pl.when(ok)(cp.wait_send)


CFG = {"step": 3.0, "lag": 7.0, "mm": 3.0}


def solution(mesh):
    n = mesh.shape["ep"]
    nz = n // 4

    def shards(tokens, expert_ids, gate_probs, w_gate, w_up, w_down):
        toks, width = tokens.shape
        ff = w_gate.shape[2]
        chunks = toks // ROWS
        half = width // 2
        bf = jnp.bfloat16
        dma = pltpu.SemaphoreType.DMA
        hbm = pl.BlockSpec(memory_space=pl.ANY)
        vmem = pl.BlockSpec(memory_space=pltpu.VMEM)
        return pl.pallas_call(
            functools.partial(kernel, n, CFG),
            out_shape=jax.ShapeDtypeStruct((toks, width), bf),
            in_specs=[hbm, vmem, vmem, hbm, hbm, hbm],
            out_specs=vmem,
            scratch_shapes=[
                pltpu.VMEM((chunks, nz, 2, 2, ROWS, width + LANES), bf),
                pltpu.VMEM((chunks, nz, 2, 2, ROWS, width), bf),
                pltpu.VMEM((chunks, 2, nz, 2, ROWS, half), bf),
                pltpu.VMEM((chunks, 2, 2, nz, 2, ROWS, half), bf),
                pltpu.VMEM((chunks, 2, ROWS, half), bf),
                pltpu.VMEM((toks, LANES), bf),
                pltpu.VMEM((n * ROWS, ff), bf),
                pltpu.VMEM((width, ff), bf),
                pltpu.VMEM((width, ff), bf),
                pltpu.VMEM((ff, width), bf),
                dma((chunks, 2)), dma((chunks, 2)),
                dma((chunks, 2, 2, nz)), dma((chunks, 2, nz)),
                dma((chunks, 2, nz)), dma((chunks, 2, nz)),
                dma((chunks, 2, nz)), dma((chunks, 2, nz)),
                dma((chunks, 2, 2, nz)), dma((chunks, 2, 2, nz)),
                dma((chunks, 2)), dma((chunks, 2)),
                dma((2 * chunks + 3,)),
            ],
            compiler_params=pltpu.CompilerParams(
                collective_id=0, has_side_effects=True, vmem_limit_bytes=60 * 1024 * 1024),
        )(tokens, expert_ids, gate_probs, w_gate, w_up, w_down)

    placed = (
        P(("dp", "ep"), None),
        P(("dp", "ep"), None),
        P(("dp", "ep"), None),
        P("ep", None, None),
        P("ep", None, None),
        P("ep", None, None),
    )
    return jax.shard_map(
        shards, mesh=mesh, in_specs=placed, out_specs=P(("dp", "ep"), None), check_vma=False
    )
```

time: 250 us -> 96 us (0.38); the launches traced: 245 us -> 95.7 us
  waiting for transfers between devices: 97.7 us -> 0 us
  Pallas kernels: 0 us -> 91.3 us
  blocking collectives: 57.1 us -> 0 us
  matrix products: 29.9 us -> 0 us
  starting transfers between devices: 27.5 us -> 0 us
  local copies, waits for them, and re-layouts: 23.2 us -> 4.42 us
  other arithmetic: 9.31 us -> 0 us
    all_to_all x3 -> x0, waiting for transfers between devices: 97.7 us -> none  [the longest x2 68 us: shards(): lax.all_to_all(served, 'ep', split_axis=0, concat_axis=0, tiled=True)]
    pallas_call x0 -> x1, Pallas kernels: none -> 91.3 us  [shards(): pl.pallas_call(functools.partial(kernel, n, CFG), out_shape=jax.ShapeDtyp...]
    all_to_all x1 -> x0, blocking collectives: 57.1 us -> none  [shards(): lax.all_to_all(part_rows, 'ep', split_axis=0, concat_axis=0, tiled=True)]
    dot_general x5 -> x0, matrix products: 29.9 us -> none  [the longest x2 16.5 us: expert_ffn(): jnp.dot(hidden, down_matrix, preferred_element_type=jnp.float32)]
    all_to_all x3 -> x0, starting transfers between devices: 27.5 us -> none  [the longest x2 22.5 us: shards(): lax.all_to_all(served, 'ep', split_axis=0, concat_axis=0, tiled=True)]
    gather x2 -> x0, local copies, waits for them, and re-layouts: 14 us -> none  [the longest x1 8 us: shards(): gathered.reshape(-1, features)[slot_index]]
    scatter x2 -> x0, local copies, waits for them, and re-layouts: 4.89 us -> none  [the longest x1 2.45 us: shards(): filled = jnp.zeros((ep_count * most,), jnp.bool_).at[slot_index].set(True)]
    concatenate x1 -> x0, other arithmetic: 4.73 us -> none  [shards(): gathered = jnp.concatenate(returned_parts, axis=1)]
  transfers between devices with their start and end apart: 3 -> 0, of which waited for: 3 -> 0; matrix products, arithmetic and copies ran while one was open for 11% -> 0% of each run, Pallas kernels for 0% -> 0%
where the time goes in v1:
time: 96 us; the launch traced here: 95.7 us
  Pallas kernels  91.3 us (95%)
  local copies, waits for them, and re-layouts  4.42 us (5%)
    pallas_call x1, Pallas kernels, shards(): pl.pallas_call(functools.partial(kernel, n, CFG), out_shape=jax.ShapeDtyp...  91.3 us
    unnamed x3, local copies, waits for them, and re-layouts  4.42 us

profile of v1, /device:TPU:0, one launch (start us, length us, event | category | flops | bytes accessed | tf_op | source)
XLA Modules:
  0.0 95.7 jit_solution(8438974624832086380)
XLA Ops:
  0.0 1.4 %copy.7.ids = s32[64,8]{1,0:T(8,128)} copy(s32[64,8]{0,1:T(8,128)} %param.7) | data formatting | bytes 4096 | tf_op args[1]
  1.4 1.4 %copy.8.probs = f32[64,8]{1,0:T(8,128)} copy(f32[64,8]{0,1:T(8,128)} %param.8) | data formatting | bytes 4096 | tf_op args[2]
  2.8 91.3 %shard_map.64 = bf16[64,2048]{1,0:T(8,128)(2,1)} custom-call(bf16[64,2048]{1,0:T(8,128)(2,1)} %tokens.1, s32[64,8]{1,0:T(8,128)} %copy.7.ids, f32[64,8]{1,0:T(8,128)} %copy.8.probs, bf16[1,2048,768]{2,1,0:T(8,128)(2,1)} %wg_hbm.1, bf16[1,2048,768]{2,1,0:T(8,128)(2,1)} %wu_hbm.1, bf16[1,768,2048]{2,1,0:T(8,128)(2,1)} %wd_hbm.1), custom_call_target="tpu_custom_call" | custom-call | tf_op jit(solution)/shard_map/pallas_call | solution.py:259
  94.0 1.7 %copy.10 = bf16[64,2048]{1,0:T(8,128)(2,1)} copy(bf16[64,2048]{1,0:T(8,128)(2,1)} %shard_map.64) | data formatting | bytes 524288

commit v2 on v1

--- a/solution.py
+++ b/solution.py
@@ -21,6 +21,8 @@
     chunks = toks // ROWS
     half = width // 2
     ff = wg.shape[1]
+    ag_z = [c for c in range(chunks) if c % cfg["ag_every"] == cfg["ag_at"]]
+    rs_z = [c for c in range(chunks) if c % cfg["rs_every"] == cfg["rs_at"]]
     me = lax.axis_index("ep")
     x, y, z = me % 2, (me // 2) % 2, me // 4
     up, down = z < nz - 1, z > 0
@@ -36,8 +38,6 @@
                                    x_buf.at[c, z, y, x, :, 0:width], loc.at[c])
         cp.start()
         own.append(cp)
-    for cp in wcopies:
-        cp.start()
 
     barrier = pltpu.get_barrier_semaphore()
     for nbr in (x_nbr, y_nbr):
@@ -48,14 +48,14 @@
             pl.semaphore_signal(barrier, inc=1, device_id=nbr, device_id_type=pl.DeviceIdType.MESH)
 
     p = probs[...]
-    w = p / jnp.sum(p, axis=1, keepdims=True)
-    lane = lax.broadcasted_iota(jnp.int32, (toks, LANES), 1)
-    named = jnp.where(lane < n, lane, lane - n)
-    g = jnp.zeros((toks, LANES), jnp.float32)
-    for k in range(ids.shape[1]):
-        g = g + jnp.where(ids[:, k:k + 1] == named, w[:, k:k + 1], 0.0)
+    w = p / jnp.sum(p, axis=0, keepdims=True)
+    row = lax.broadcasted_iota(jnp.int32, (LANES, toks), 0)
+    named = jnp.where(row < n, row, row - n)
+    g = jnp.zeros((LANES, toks), jnp.float32)
+    for k in range(ids.shape[0]):
+        g = g + jnp.where(ids[k:k + 1, :] == named, w[k:k + 1, :], 0.0)
     hi = g.astype(jnp.bfloat16).astype(jnp.float32)
-    gates[...] = jnp.where(lane < n, hi, g - hi).astype(jnp.bfloat16)
+    gates[...] = jnp.transpose(jnp.where(row < n, hi, g - hi)).astype(jnp.bfloat16)
     gcopies = []
     for c in range(chunks):
         cp = pltpu.make_async_copy(gates.at[c * ROWS:(c + 1) * ROWS],
@@ -88,35 +88,54 @@
             return buf.at[c, zz, (1 - y) if other else y, :, :, cs[0]]
         return buf.at[c, zz, :, (1 - x) if other else x, :, cs[1]]
 
+    def mate(buf, c, h, zz, cs):
+        return buf.at[c, zz, y, 1 - x, :, cs[0]] if h == 0 else buf.at[c, zz, 1 - y, x, :, cs[1]]
+
+    def mine(buf, c, h, zz, cs):
+        return buf.at[c, zz, y, x, :, cs[h]]
+
     def ag_first(c):
         own[c].wait()
         gcopies[c].wait()
-        for h in range(2):
-            blk = x_buf.at[c, z, y, x, :, cols[h]]
-            send(blk, blk, ag1_s.at[c, h], ag1_r.at[c, h], first_nbr[h])
+        if c not in ag_z:
+            for h in range(2):
+                ag_pair(c, h, z)
+
+    def ag_pair(c, h, zz, ok=None):
+        blk = mine(x_buf, c, h, zz, cols)
+        send(blk, blk, ag1_s.at[c, h, zz], ag1_r.at[c, h, zz], first_nbr[h], ok)
 
     def ag_last(c, h, zz, ok=None):
         blk = group(x_buf, c, h, zz, cols)
         send(blk, blk, ag3_s.at[c, h, zz], ag3_r.at[c, h, zz], last_nbr[h], ok)
 
     def ag_step(c, d):
+        part = mine if c in ag_z else group
+        spread = ag_pair if c in ag_z else ag_last
         for h in range(2):
             if d == 0:
-                mate = (x_buf.at[c, z, y, 1 - x, :, cols[0]], x_buf.at[c, z, 1 - y, x, :, cols[1]])[h]
-                landed(mate, ag1_r.at[c, h])
-                blk = group(x_buf, c, h, z, cols)
+                if c not in ag_z:
+                    landed(mate(x_buf, c, h, z, cols), ag1_r.at[c, h, z])
+                blk = part(x_buf, c, h, z, cols)
                 send(blk, blk, agz_s.at[c, h, 0, z], agz_r.at[c, h, z], up_nbr, up)
                 send(blk, blk, agz_s.at[c, h, 1, z], agz_r.at[c, h, z], down_nbr, down)
-                ag_last(c, h, z)
+                spread(c, h, z)
             else:
                 for way, origin, ok, more, nbr in ((0, z - d, z - d >= 0, up, up_nbr),
                                                    (1, z + d, z + d <= nz - 1, down, down_nbr)):
                     at = jnp.clip(origin, 0, nz - 1)
-                    blk = group(x_buf, c, h, at, cols)
+                    blk = part(x_buf, c, h, at, cols)
                     pl.when(ok)(functools.partial(landed, blk, agz_r.at[c, h, at]))
                     if d < nz - 1:
                         send(blk, blk, agz_s.at[c, h, way, at], agz_r.at[c, h, at], nbr, jnp.logical_and(ok, more))
-                    ag_last(c, h, at, ok)
+                    spread(c, h, at, ok)
+
+    def ag_mid(c, d):
+        for h in range(2):
+            for origin, ok in ((z - d, z - d >= 0), (z + d, z + d <= nz - 1))[:2 if d else 1]:
+                at = jnp.clip(origin, 0, nz - 1)
+                pl.when(ok)(functools.partial(landed, mate(x_buf, c, h, at, cols), ag1_r.at[c, h, at]))
+                ag_last(c, h, at, ok)
 
     def ag_end(c):
         for h in range(2):
@@ -163,60 +182,89 @@
             send(group(y_buf, c, h, zz, ycols, True), r1.at[c, h, zz], rs1_s.at[c, h, zz],
                  rs1_r.at[c, h, zz], last_nbr[h])
 
-    def add(c, h, zz, bufs):
-        mine = group(y_buf, c, h, zz, ycols)
-        total = mine[...].astype(jnp.float32)
+    def add(place, bufs):
+        total = place[...].astype(jnp.float32)
         for b in bufs:
             total = total + b[...].astype(jnp.float32)
-        mine[...] = total.astype(jnp.bfloat16)
+        place[...] = total.astype(jnp.bfloat16)
+
+    def rs_mid(c, s):
+        k = nz - 1 - s
+        for h in range(2):
+            for dest, ok in ((z + k, z + k <= nz - 1), (z - k, z - k >= 0))[:2 if k else 1]:
+                at = jnp.clip(dest, 0, nz - 1)
+
+                @pl.when(ok)
+                def _():
+                    landed(r1.at[c, h, at], rs1_r.at[c, h, at])
+                    add(group(y_buf, c, h, at, ycols), (r1.at[c, h, at],))
+
+                send(mate(y_buf, c, h, at, ycols), r3.at[c, h, at], rs3_s.at[c, h, at],
+                     rs3_r.at[c, h, at], first_nbr[h], ok)
 
     def rs_step(c, s):
         k = nz - 1 - s
+        part = mine if c in rs_z else group
+        before = (r3, rs3_r) if c in rs_z else (r1, rs1_r)
+        hop = lambda h, way, at: r2.at[c, h, way, at, 0] if c in rs_z else r2.at[c, h, way, at]
         for h in range(2):
             if k > 0:
                 for way, dest, ok, prev, nbr in ((0, z + k, z + k <= nz - 1, down, up_nbr),
                                                  (1, z - k, z - k >= 0, up, down_nbr)):
                     at = jnp.clip(dest, 0, nz - 1)
+                    place, buf = part(y_buf, c, h, at, ycols), before[0].at[c, h, at]
 
                     @pl.when(ok)
                     def _():
-                        landed(r1.at[c, h, at], rs1_r.at[c, h, at])
+                        landed(buf, before[1].at[c, h, at])
 
                         @pl.when(prev)
                         def _():
-                            landed(r2.at[c, h, way, at], rs2_r.at[c, h, way, at])
-                            add(c, h, at, (r1.at[c, h, at], r2.at[c, h, way, at]))
+                            landed(hop(h, way, at), rs2_r.at[c, h, way, at])
+                            add(place, (buf, hop(h, way, at)))
 
                         @pl.when(jnp.logical_not(prev))
                         def _():
-                            add(c, h, at, (r1.at[c, h, at],))
-
-                    send(group(y_buf, c, h, at, ycols), r2.at[c, h, way, at], rs2_s.at[c, h, way, at],
+                            add(place, (buf,))
+
+                    send(place, hop(h, way, at), rs2_s.at[c, h, way, at],
                          rs2_r.at[c, h, way, at], nbr, ok)
             else:
-                landed(r1.at[c, h, z], rs1_r.at[c, h, z])
-                add(c, h, z, (r1.at[c, h, z],))
+                place = part(y_buf, c, h, z, ycols)
+                landed(before[0].at[c, h, z], before[1].at[c, h, z])
+                add(place, (before[0].at[c, h, z],))
                 for way, prev in ((0, down), (1, up)):
                     @pl.when(prev)
                     def _():
-                        landed(r2.at[c, h, way, z], rs2_r.at[c, h, way, z])
-                        add(c, h, z, (r2.at[c, h, way, z],))
-                mate = (y_buf.at[c, z, y, 1 - x, :, ycols[0]], y_buf.at[c, z, 1 - y, x, :, ycols[1]])[h]
-                send(mate, r3.at[c, h], rs3_s.at[c, h], rs3_r.at[c, h], first_nbr[h])
+                        landed(hop(h, way, z), rs2_r.at[c, h, way, z])
+                        add(place, (hop(h, way, z),))
+                if c in rs_z:
+                    out[c * ROWS:(c + 1) * ROWS, ycols[h]] = place[...]
+                else:
+                    send(mate(y_buf, c, h, z, ycols), r3.at[c, h, z], rs3_s.at[c, h, z],
+                         rs3_r.at[c, h, z], first_nbr[h])
 
     def rs_end(c):
         for h in range(2):
-            landed(r3.at[c, h], rs3_r.at[c, h])
-            total = y_buf[c, z, y, x, :, ycols[h]].astype(jnp.float32) + r3[c, h].astype(jnp.float32)
+            landed(r3.at[c, h, z], rs3_r.at[c, h, z])
+            total = mine(y_buf, c, h, z, ycols)[...].astype(jnp.float32) + r3[c, h, z].astype(jnp.float32)
             out[c * ROWS:(c + 1) * ROWS, ycols[h]] = total.astype(jnp.bfloat16)
 
-    tasks = []
-    step, lag, mm = cfg["step"], cfg["lag"], cfg["mm"]
+    def weights():
+        for cp in wcopies:
+            cp.start()
+
+    tasks = [(-8.995, weights)]
+    step, lag, mm, rlag = cfg["step"], cfg["lag"], cfg["mm"], cfg["rlag"]
     for c in range(chunks):
-        tasks.append((-1.0 + c * 0.01, functools.partial(ag_first, c)))
+        tasks.append((-9.0 + c * 0.01, functools.partial(ag_first, c)))
         t = c * lag
         for d in range(nz):
-            tasks.append((t, functools.partial(ag_step, c, d)))
+            if c in ag_z:
+                tasks.append((t - step, functools.partial(ag_step, c, d)))
+                tasks.append((t, functools.partial(ag_mid, c, d)))
+            else:
+                tasks.append((t, functools.partial(ag_step, c, d)))
             t += step
         tasks.append((t, functools.partial(ag_end, c)))
         tasks.append((t + 0.01, functools.partial(ffn_in, c)))
@@ -225,11 +273,16 @@
             tasks.append((t + 0.01, functools.partial(ffn_out, c, part, 2)))
             tasks.append((t + 0.02, functools.partial(rs_first, c, part)))
             t += mm / 4
-        t += step
+        t += cfg["wait"] + c * (rlag - lag)
         for s in range(nz):
-            tasks.append((t, functools.partial(rs_step, c, s)))
+            if c in rs_z:
+                tasks.append((t, functools.partial(rs_mid, c, s)))
+                tasks.append((t + step, functools.partial(rs_step, c, s)))
+            else:
+                tasks.append((t, functools.partial(rs_step, c, s)))
             t += step
-        tasks.append((t, functools.partial(rs_end, c)))
+        if c not in rs_z:
+            tasks.append((t, functools.partial(rs_end, c)))
     for _, task in sorted(tasks, key=lambda item: item[0]):
         task()
 
@@ -240,7 +293,7 @@
             pl.when(ok)(cp.wait_send)
 
 
-CFG = {"step": 3.0, "lag": 7.0, "mm": 3.0}
+CFG = {"step": 3.0, "lag": 5.0, "mm": 3.0, "rlag": 5.0, "wait": 3.0, "ag_every": 4, "ag_at": 0, "rs_every": 4, "rs_at": 3}
 
 
 def solution(mesh):
@@ -266,23 +319,23 @@
                 pltpu.VMEM((chunks, nz, 2, 2, ROWS, width), bf),
                 pltpu.VMEM((chunks, 2, nz, 2, ROWS, half), bf),
                 pltpu.VMEM((chunks, 2, 2, nz, 2, ROWS, half), bf),
-                pltpu.VMEM((chunks, 2, ROWS, half), bf),
+                pltpu.VMEM((chunks, 2, nz, ROWS, half), bf),
                 pltpu.VMEM((toks, LANES), bf),
                 pltpu.VMEM((n * ROWS, ff), bf),
                 pltpu.VMEM((width, ff), bf),
                 pltpu.VMEM((width, ff), bf),
                 pltpu.VMEM((ff, width), bf),
-                dma((chunks, 2)), dma((chunks, 2)),
+                dma((chunks, 2, nz)), dma((chunks, 2, nz)),
                 dma((chunks, 2, 2, nz)), dma((chunks, 2, nz)),
                 dma((chunks, 2, nz)), dma((chunks, 2, nz)),
                 dma((chunks, 2, nz)), dma((chunks, 2, nz)),
                 dma((chunks, 2, 2, nz)), dma((chunks, 2, 2, nz)),
-                dma((chunks, 2)), dma((chunks, 2)),
+                dma((chunks, 2, nz)), dma((chunks, 2, nz)),
                 dma((2 * chunks + 3,)),
             ],
             compiler_params=pltpu.CompilerParams(
                 collective_id=0, has_side_effects=True, vmem_limit_bytes=60 * 1024 * 1024),
-        )(tokens, expert_ids, gate_probs, w_gate, w_up, w_down)
+        )(tokens, expert_ids.T, gate_probs.T, w_gate, w_up, w_down)
 
     placed = (
         P(("dp", "ep"), None),

time: 96 us -> 88.5 us (0.922)
  Pallas kernels: 91.3 us -> 86.7 us
  local copies, waits for them, and re-layouts: 4.42 us -> 1.67 us
    pallas_call x1, Pallas kernels: 91.3 us -> 86.7 us  [shards(): pl.pallas_call(functools.partial(kernel, n, CFG), out_shape=jax.ShapeDtyp...]
    unnamed x3 -> x1, local copies, waits for them, and re-layouts: 4.42 us -> 1.67 us
where the time goes in v2:
time: 88.5 us; the launch traced here: 88.3 us
  Pallas kernels  86.7 us (98%)
  local copies, waits for them, and re-layouts  1.67 us (2%)
    pallas_call x1, Pallas kernels, shards(): pl.pallas_call(functools.partial(kernel, n, CFG), out_shape=jax.ShapeDtyp...  86.7 us

profile of v2, /device:TPU:0, one launch (start us, length us, event | category | flops | bytes accessed | tf_op | source)
XLA Modules:
  0.0 88.3 jit_solution(14047846520114270425)
XLA Ops:
  0.0 86.7 %shard_map.64 = bf16[64,2048]{1,0:T(8,128)(2,1)} custom-call(bf16[64,2048]{1,0:T(8,128)(2,1)} %tokens.1, s32[8,64]{1,0:T(8,128)} %bitcast.2, f32[8,64]{1,0:T(8,128)} %bitcast.3, bf16[1,2048,768]{2,1,0:T(8,128)(2,1)} %wg_hbm.1, bf16[1,2048,768]{2,1,0:T(8,128)(2,1)} %wu_hbm.1, bf16[1,768,2048]{2,1,0:T(8,128)(2,1)} %wd_hbm.1), custom_call_target="tpu_custom_call" | custom-call | tf_op jit(solution)/shard_map/pallas_call | solution.py:312
  86.7 1.7 %copy.8 = bf16[64,2048]{1,0:T(8,128)(2,1)} copy(bf16[64,2048]{1,0:T(8,128)(2,1)} %shard_map.64) | data formatting | bytes 524288

commit v3 on v2

--- a/solution.py
+++ b/solution.py
@@ -293,7 +293,7 @@
             pl.when(ok)(cp.wait_send)
 
 
-CFG = {"step": 3.0, "lag": 5.0, "mm": 3.0, "rlag": 5.0, "wait": 3.0, "ag_every": 4, "ag_at": 0, "rs_every": 4, "rs_at": 3}
+CFG = {"step": 3.0, "lag": 5.0, "mm": 3.0, "rlag": 4.0, "wait": 3.0, "ag_every": 4, "ag_at": 0, "rs_every": 4, "rs_at": 3}
 
 
 def solution(mesh):

time: 88.5 us -> 86.6 us (0.979)
  Pallas kernels: 86.7 us -> 84.8 us
    pallas_call x1, Pallas kernels: 86.7 us -> 84.8 us  [shards(): pl.pallas_call(functools.partial(kernel, n, CFG), out_shape=jax.ShapeDtyp...]
where the time goes in v3:
time: 86.6 us; the launch traced here: 86.4 us
  Pallas kernels  84.8 us (98%)
  local copies, waits for them, and re-layouts  1.67 us (2%)
    pallas_call x1, Pallas kernels, shards(): pl.pallas_call(functools.partial(kernel, n, CFG), out_shape=jax.ShapeDtyp...  84.8 us

profile of v3, /device:TPU:0, one launch (start us, length us, event | category | flops | bytes accessed | tf_op | source)
XLA Modules:
  0.0 86.4 jit_solution(11827981412265768210)
XLA Ops:
  0.0 84.8 %shard_map.64 = bf16[64,2048]{1,0:T(8,128)(2,1)} custom-call(bf16[64,2048]{1,0:T(8,128)(2,1)} %tokens.1, s32[8,64]{1,0:T(8,128)} %bitcast.2, f32[8,64]{1,0:T(8,128)} %bitcast.3, bf16[1,2048,768]{2,1,0:T(8,128)(2,1)} %wg_hbm.1, bf16[1,2048,768]{2,1,0:T(8,128)(2,1)} %wu_hbm.1, bf16[1,768,2048]{2,1,0:T(8,128)(2,1)} %wd_hbm.1), custom_call_target="tpu_custom_call" | custom-call | tf_op jit(solution)/shard_map/pallas_call | solution.py:312
  84.8 1.7 %copy.8 = bf16[64,2048]{1,0:T(8,128)(2,1)} copy(bf16[64,2048]{1,0:T(8,128)(2,1)} %shard_map.64) | data formatting | bytes 524288
